TPU v7x, 512 devices: a whole 4x8x8 slice. The times are simulated.
512 devices in a mesh: pipe: 2 (over core), tensor: 8 (over x, y_hi), expert: 32 (over y_lo, z).
Axes of the slice: x: 4, y: 8 (y_hi: 2, y_lo: 4; y = y_hi * 4 + y_lo), z: 8, core: 2. Of those that a mesh axis runs over, the one named last changes fastest.
Arguments:
- tokens: bfloat16 [3, 1536, 4096], P(None, 'expert', 'tensor'), may hold values from -36 to 36
- norm_gain: float32 [2, 4096], P('pipe'), may hold values from 0.1 to 1.9
- shared_gate: bfloat16 [2, 4096, 1024], P('pipe', 'expert', 'tensor'), may hold values from -0.09375 to 0.09375
- shared_up: bfloat16 [2, 4096, 1024], P('pipe', 'expert', 'tensor'), may hold values from -0.09375 to 0.09375
- shared_down: bfloat16 [2, 1024, 4096], P('pipe', 'tensor', 'expert'), may hold values from -0.1875 to 0.1875
- expert_gate: bfloat16 [2, 32, 4096, 1024], P('pipe', 'expert', None, 'tensor'), may hold values from -0.09375 to 0.09375
- expert_up: bfloat16 [2, 32, 4096, 1024], P('pipe', 'expert', None, 'tensor'), may hold values from -0.09375 to 0.09375
- expert_down: bfloat16 [2, 32, 1024, 4096], P('pipe', 'expert', 'tensor'), may hold values from -0.1875 to 0.1875
- expert_ids: int32 [2, 3, 1536, 8], P('pipe', None, 'expert'), may hold values from 0 to 255, as said below
- expert_slots: int32 [2, 3, 1536, 8], P('pipe', None, 'expert'), may hold values from -1 to 2, as said below
- route_weights: float32 [2, 3, 1536, 8], P('pipe', None, 'expert'), may hold values from 0.1 to 1
Outputs:
- states: bfloat16 [2, 3, 1536, 4096], P('pipe', None, 'expert', 'tensor')
Inputs may be any that keep to these rules, and one draw needn't show every extreme that they name: `expert_ids`: the 8 ids of a token are distinct. Ids of 32 and above name experts that are not held and add nothing. `expert_slots`: for a choice whose id is below 32: the number of earlier choices (earlier tokens, or lower k of the same token) of the same block of 48 tokens, same layer and microbatch, that name the same expert, if that number is below 3; otherwise -1. For ids of 32 and above: -1.
All inputs are finite; a program needn't handle non-finite values.
Results may differ from a plain program's by a relative error of at most 0.0085.
Values may be sent and summed in bfloat16 or wider, within the bound.
No kernel may reach another device: no remote copies, remote signals or barrier semaphores. Data moves between devices by JAX's collectives and lax.ppermute only.
A program may use at most 64 MiB of HBM per device.

v0:
```python
import jax
import jax.numpy as jnp
from jax import lax
from jax.sharding import PartitionSpec as P

CAP = 3


def turned_gather(arrays, axis, dims):
    turned = [jnp.moveaxis(a, dim, 0) for a, dim in zip(arrays, dims)]
    both = jnp.concatenate([t.reshape(len(t), -1) for t in turned], axis=1)
    filled, at, outs = (lax.all_gather(both, axis, axis=0, tiled=True), 0, [])
    for t, dim in zip(turned, dims):
        share = filled[:, at : at + t[0].size].reshape(-1, *t.shape[1:])
        outs.append(jnp.moveaxis(share, 0, dim))
        at += t[0].size
    return tuple(outs)


def laid_out(blocks, dim):
    shape = list(blocks.shape[1:])
    shape[dim] *= blocks.shape[0]
    return jnp.moveaxis(blocks, 0, dim).reshape(shape)


def from_everyone(x, axis):
    copies = jnp.broadcast_to(x, (lax.axis_size(axis), *x.shape))
    return lax.all_to_all(copies, axis, split_axis=0, concat_axis=0, tiled=True)


def gather_directly(x, axis, dim):
    return laid_out(from_everyone(x, axis), dim)


def in_blocks(x, dim, peers):
    shape = x.shape
    blocks = x.reshape(*shape[:dim], peers, shape[dim] // peers, *shape[dim + 1 :])
    return jnp.moveaxis(blocks, dim, 0)


def sent_and_summed(x, axis, dim):
    blocks = in_blocks(x, dim, lax.axis_size(axis))
    arrived = lax.all_to_all(blocks, axis, split_axis=0, concat_axis=0, tiled=True)
    return arrived.astype(jnp.float32).sum(axis=0)


def from_behind(value, axis, steps):
    count = lax.axis_size(axis)
    initial, last = (max(0, -steps), min(count, count - steps))
    return lax.ppermute(value, axis, [(source, source + steps) for source in range(initial, last)])


def product(left, right):
    return jnp.dot(left, right, preferred_element_type=jnp.float32)


def per_device(
    tokens,
    norm_gain,
    shared_gate,
    shared_up,
    shared_down,
    expert_gate,
    expert_up,
    expert_down,
    expert_ids,
    expert_slots,
    route_weights,
):
    section_index = lax.axis_index("pipe")
    n_experts = lax.axis_size("expert")
    n_tensor = lax.axis_size("tensor")
    batches = tokens.shape[0]
    shard_rows = tokens.shape[1]
    slice_width = tokens.shape[2]
    model_width = slice_width * n_tensor
    capacity = CAP
    slot_total = n_experts * capacity
    slot_range = jnp.arange(slot_total, dtype=jnp.int32)
    shared_gate_full, shared_up_full, shared_down_full = turned_gather(
        (shared_gate[0], shared_up[0], shared_down[0]), "expert", (0, 0, 1)
    )
    local_gate = expert_gate[0, 0]
    local_up = expert_up[0, 0]
    local_down = expert_down[0, 0]
    layer_gain = norm_gain[0]
    incoming = jnp.zeros((shard_rows, slice_width), jnp.bfloat16)
    produced = []
    for step_index in range(batches + 1):
        fresh_rows = tokens[min(step_index, batches - 1)]
        current = jnp.where(section_index == 0, fresh_rows, incoming)
        batch_index = jnp.clip(step_index - section_index, 0, batches - 1)
        route_ids = lax.dynamic_index_in_dim(expert_ids[0], batch_index, 0, keepdims=False)
        slot_rank = lax.dynamic_index_in_dim(expert_slots[0], batch_index, 0, keepdims=False)
        weights = lax.dynamic_index_in_dim(route_weights[0], batch_index, 0, keepdims=False)
        full_rows = gather_directly(current, "tensor", 1)
        values = full_rows.astype(jnp.float32)
        inverse_rms = lax.rsqrt(jnp.mean(values * values, axis=-1, keepdims=True) + 1e-06)
        normed = (values * inverse_rms * layer_gain).astype(jnp.bfloat16)
        shared_hidden = (
            jax.nn.silu(product(normed, shared_gate_full)) * product(normed, shared_up_full)
        ).astype(jnp.bfloat16)
        partial_value = product(shared_hidden, shared_down_full)
        valid = (route_ids < n_experts) & (slot_rank >= 0)
        slot_code = jnp.where(valid, route_ids * capacity + slot_rank, -1)
        matched = slot_code[:, :, None] == slot_range[None, None, :]
        picker = jnp.any(matched, axis=1).T.astype(jnp.bfloat16)
        combine = jnp.sum(jnp.where(matched, weights[:, :, None], jnp.float32(0.0)), axis=1)
        outgoing = (
            product(picker, normed).astype(jnp.bfloat16).reshape(n_experts, capacity, model_width)
        )
        arrived = lax.all_to_all(
            outgoing, "expert", split_axis=0, concat_axis=0, tiled=True
        ).reshape(slot_total, model_width)
        gate_rows = product(arrived, local_gate)
        up_rows = product(arrived, local_up)
        expert_hidden = (jax.nn.silu(gate_rows) * up_rows).astype(jnp.bfloat16)
        outcome = (
            product(expert_hidden, local_down)
            .astype(jnp.bfloat16)
            .reshape(n_experts, capacity, model_width)
        )
        returned = lax.all_to_all(
            outcome, "expert", split_axis=0, concat_axis=0, tiled=True
        ).reshape(slot_total, model_width)
        routed = jnp.dot(combine, returned.astype(jnp.float32), preferred_element_type=jnp.float32)
        summed = sent_and_summed((partial_value + routed).astype(jnp.bfloat16), "tensor", 1)
        result = (current.astype(jnp.float32) + summed).astype(jnp.bfloat16)
        produced.append(result)
        if step_index < batches:
            incoming = from_behind(result, "pipe", 1)
    outputs = [
        jnp.where(section_index == 0, produced[index_now], produced[index_now + 1])
        for index_now in range(batches)
    ]
    return jnp.stack(outputs)[None]


def solution(mesh):
    in_specs = (
        P(None, "expert", "tensor"),
        P("pipe", None),
        P("pipe", "expert", "tensor"),
        P("pipe", "expert", "tensor"),
        P("pipe", "tensor", "expert"),
        P("pipe", "expert", None, "tensor"),
        P("pipe", "expert", None, "tensor"),
        P("pipe", "expert", "tensor", None),
        P("pipe", None, "expert", None),
        P("pipe", None, "expert", None),
        P("pipe", None, "expert", None),
    )
    out_specs = P("pipe", None, "expert", "tensor")
    return jax.shard_map(
        per_device, mesh=mesh, in_specs=in_specs, out_specs=out_specs, check_vma=False
    )
```

profile of v0, /device:TPU:72, one launch (start us, length us, event | category | flops | bytes accessed | tf_op | source)
XLA Modules:
  0.0 615.7 jit_solution(16635909837770484328)
XLA Ops:
  8.2 8.7 %all-to-all-start = ((bf16[8,48,512]{2,1,0:T(8,128)(2,1)}), bf16[8,48,512]{2,1,0:T(8,128)(2,1)S(1)}, u32[]{:S(2)}, u32[]{:S(2)}) async-start(bf16[8,48,512]{2,1,0:T(8,128)(2,1)} %broadcast_in_dim.80), calls=%async_computation | async-start | bytes 786432 | tf_op jit(solution)/shard_map/all_to_all | solution.py:28
  20.1 1.4 select_bitcast_fusion.3
  21.8 11.9 %all-to-all-done = bf16[8,48,512]{2,1,0:T(8,128)(2,1)S(1)} async-done(((bf16[8,48,512]{2,1,0:T(8,128)(2,1)}), bf16[8,48,512]{2,1,0:T(8,128)(2,1)S(1)}, u32[]{:S(2)}, u32[]{:S(2)}) %all-to-all-start) | async-done | bytes 393248 | tf_op jit(solution)/shard_map/all_to_all | solution.py:28
  36.0 39.3 %all_to_all.80 = bf16[32,3,4096]{2,1,0:T(4,128)(2,1)} all-to-all(bf16[32,3,4096]{2,1,0:T(4,128)(2,1)} %reshape.259), channel_id=1, replica_groups=mesh['pipe'=2,'tensor'=8,'expert'=32] {'expert'}, dimensions={0} | all-to-all | bytes 1572864 | tf_op jit(solution)/shard_map/all_to_all | solution.py:112
  75.3 2.5 reshape.260
  77.7 2.1 fusion.34
  79.8 2.7 convolution_convert_fusion.3
  82.6 2.3 reshape.261
  84.8 8.4 %all-to-all-start.2 = ((bf16[32,3,4096]{2,1,0:T(4,128)(2,1)}), bf16[32,3,4096]{2,1,0:T(4,128)(2,1)}, u32[]{:S(2)}, u32[]{:S(2)}) async-start(bf16[32,3,4096]{2,1,0:T(4,128)(2,1)} %reshape.261), calls=%async_computation.2 | async-start | bytes 2097152 | tf_op jit(solution)/shard_map/all_to_all | solution.py:123
  96.0 1.5 select_reduce_fusion.3
  97.6 22.4 %all-to-all-done.2 = bf16[32,3,4096]{2,1,0:T(4,128)(2,1)} async-done(((bf16[32,3,4096]{2,1,0:T(4,128)(2,1)}), bf16[32,3,4096]{2,1,0:T(4,128)(2,1)}, u32[]{:S(2)}, u32[]{:S(2)}) %all-to-all-start.2) | async-done | bytes 786464 | tf_op jit(solution)/shard_map/all_to_all | solution.py:123
  120.0 2.5 reshape.262
  122.4 74.5 %all-gather.2.cloned.1.call-done = bf16[4096,384]{0,1:T(8,128)(2,1)} async-done(((bf16[128,384]{0,1:T(8,128)(2,1)}), bf16[4096,384]{0,1:T(8,128)(2,1)}) %all-gather.2.cloned.1.call-update) | async-done | bytes 3145744 | tf_op jit(solution)/shard_map/all_gather | solution.py:12
  196.9 2.3 fusion.58
  199.2 3.4 fusion.15
  202.5 1.7 fusion
  204.3 17.6 %all_to_all.81 = bf16[8,48,512]{2,1,0:T(8,128)(2,1)S(1)} all-to-all(bf16[8,48,512]{2,1,0:T(8,128)(2,1)S(1)} %bitcast.150), channel_id=1, replica_groups=mesh['pipe'=2,'tensor'=8,'expert'=32] {'tensor'}, dimensions={0} | all-to-all | bytes 786432 | tf_op jit(solution)/shard_map/all_to_all | solution.py:43
  225.6 3.5 all-to-all-start.4
  230.4 1.5 fusion.62
  231.9 12.8 %all-to-all-done.4 = bf16[8,48,512]{2,1,0:T(8,128)(2,1)S(1)} async-done(((bf16[8,48,512]{2,1,0:T(8,128)(2,1)}), bf16[8,48,512]{2,1,0:T(8,128)(2,1)S(1)}, u32[]{:S(2)}, u32[]{:S(2)}) %all-to-all-start.4) | async-done | bytes 393248 | tf_op jit(solution)/shard_map/all_to_all | solution.py:28
  246.7 2.3 reshape.264
  248.9 39.0 %all_to_all.82 = bf16[32,3,4096]{2,1,0:T(4,128)(2,1)} all-to-all(bf16[32,3,4096]{2,1,0:T(4,128)(2,1)} %reshape.264), channel_id=1, replica_groups=mesh['pipe'=2,'tensor'=8,'expert'=32] {'expert'}, dimensions={0} | all-to-all | bytes 1572864 | tf_op jit(solution)/shard_map/all_to_all | solution.py:112
  288.0 2.5 reshape.265
  290.4 2.1 fusion.32
  292.5 2.8 convolution_convert_fusion.2
  295.3 2.3 reshape.266
  297.6 5.5 all-to-all-start.6
  304.4 1.5 select_reduce_fusion.2
  306.0 2.3 fusion.56
  308.3 3.4 fusion.14
  311.7 19.5 %all-to-all-done.6 = bf16[32,3,4096]{2,1,0:T(4,128)(2,1)} async-done(((bf16[32,3,4096]{2,1,0:T(4,128)(2,1)}), bf16[32,3,4096]{2,1,0:T(4,128)(2,1)}, u32[]{:S(2)}, u32[]{:S(2)}) %all-to-all-start.6) | async-done | bytes 786464 | tf_op jit(solution)/shard_map/all_to_all | solution.py:123
  331.2 2.5 reshape.267
  333.7 1.6 fusion.1
  335.3 20.7 %all_to_all.83 = bf16[8,48,512]{2,1,0:T(8,128)(2,1)S(1)} all-to-all(bf16[8,48,512]{2,1,0:T(8,128)(2,1)S(1)} %bitcast.151), channel_id=1, replica_groups=mesh['pipe'=2,'tensor'=8,'expert'=32] {'tensor'}, dimensions={0} | all-to-all | bytes 786432 | tf_op jit(solution)/shard_map/all_to_all | solution.py:43
  361.1 3.6 all-to-all-start.8
  366.1 1.5 fusion.61
  367.6 12.8 %all-to-all-done.8 = bf16[8,48,512]{2,1,0:T(8,128)(2,1)S(1)} async-done(((bf16[8,48,512]{2,1,0:T(8,128)(2,1)}), bf16[8,48,512]{2,1,0:T(8,128)(2,1)S(1)}, u32[]{:S(2)}, u32[]{:S(2)}) %all-to-all-start.8) | async-done | bytes 393248 | tf_op jit(solution)/shard_map/all_to_all | solution.py:28
  382.3 2.3 reshape.269
  384.6 33.6 %all_to_all.84 = bf16[32,3,4096]{2,1,0:T(4,128)(2,1)} all-to-all(bf16[32,3,4096]{2,1,0:T(4,128)(2,1)} %reshape.269), channel_id=1, replica_groups=mesh['pipe'=2,'tensor'=8,'expert'=32] {'expert'}, dimensions={0} | all-to-all | bytes 1572864 | tf_op jit(solution)/shard_map/all_to_all | solution.py:112
  418.2 2.5 reshape.270
  420.6 2.1 fusion.30
  422.7 2.8 convolution_convert_fusion.1
  425.5 2.3 reshape.271
  427.8 5.4 all-to-all-start.10
  434.5 1.5 select_reduce_fusion.1
  436.0 2.3 fusion.54
  438.3 3.4 fusion.13
  441.8 19.5 %all-to-all-done.10 = bf16[32,3,4096]{2,1,0:T(4,128)(2,1)} async-done(((bf16[32,3,4096]{2,1,0:T(4,128)(2,1)}), bf16[32,3,4096]{2,1,0:T(4,128)(2,1)}, u32[]{:S(2)}, u32[]{:S(2)}) %all-to-all-start.10) | async-done | bytes 786464 | tf_op jit(solution)/shard_map/all_to_all | solution.py:123
  461.2 2.5 reshape.272
  463.7 1.6 fusion.2
  465.4 17.9 %all_to_all.85 = bf16[8,48,512]{2,1,0:T(8,128)(2,1)S(1)} all-to-all(bf16[8,48,512]{2,1,0:T(8,128)(2,1)S(1)} %bitcast.152), channel_id=1, replica_groups=mesh['pipe'=2,'tensor'=8,'expert'=32] {'tensor'}, dimensions={0} | all-to-all | bytes 786432 | tf_op jit(solution)/shard_map/all_to_all | solution.py:43
  488.4 3.5 all-to-all-start.12
  493.2 1.5 fusion.60
  494.7 12.9 %all-to-all-done.12 = bf16[8,48,512]{2,1,0:T(8,128)(2,1)S(1)} async-done(((bf16[8,48,512]{2,1,0:T(8,128)(2,1)}), bf16[8,48,512]{2,1,0:T(8,128)(2,1)S(1)}, u32[]{:S(2)}, u32[]{:S(2)}) %all-to-all-start.12) | async-done | bytes 393248 | tf_op jit(solution)/shard_map/all_to_all | solution.py:28
  509.6 2.3 reshape.274
  511.8 35.0 %all_to_all.86 = bf16[32,3,4096]{2,1,0:T(4,128)(2,1)} all-to-all(bf16[32,3,4096]{2,1,0:T(4,128)(2,1)} %reshape.274), channel_id=1, replica_groups=mesh['pipe'=2,'tensor'=8,'expert'=32] {'expert'}, dimensions={0} | all-to-all | bytes 1572864 | tf_op jit(solution)/shard_map/all_to_all | solution.py:112
  546.8 2.5 reshape.275
  549.3 2.1 fusion.28
  551.4 1.8 convolution_convert_fusion
  554.5 5.4 all-to-all-start.14
  560.2 1.7 fusion.52
  561.9 3.3 fusion.12
  565.3 22.7 %all-to-all-done.14 = bf16[32,3,4096]{2,1,0:T(4,128)(2,1)S(1)} async-done(((bf16[32,3,4096]{2,1,0:T(4,128)(2,1)}), bf16[32,3,4096]{2,1,0:T(4,128)(2,1)S(1)}, u32[]{:S(2)}, u32[]{:S(2)}) %all-to-all-start.14) | async-done | bytes 786464 | tf_op jit(solution)/shard_map/all_to_all | solution.py:123
  590.1 17.9 %all_to_all.87 = bf16[8,48,512]{2,1,0:T(8,128)(2,1)S(1)} all-to-all(bf16[8,48,512]{2,1,0:T(8,128)(2,1)S(1)} %bitcast.153), channel_id=1, replica_groups=mesh['pipe'=2,'tensor'=8,'expert'=32] {'tensor'}, dimensions={0} | all-to-all | bytes 786432 | tf_op jit(solution)/shard_map/all_to_all | solution.py:43
  (121 shorter events, 41.0 us)
Async XLA Ops:
  6.5 73.3 %copy-start = (bf16[1,1,128,4096]{3,2,1,0:T(8,128)(2,1)S(1)}, bf16[1,1,128,4096]{3,2,1,0:T(8,128)(2,1)}, u32[]{:S(2)}) copy-start(bf16[1,1,128,4096]{3,2,1,0:T(8,128)(2,1)} %param.18) | copy-start | bytes 3145732
  6.5 27.5 %copy-start.10 = (f32[1,4096]{1,0:T(1,128)S(1)}, f32[1,4096]{1,0:T(1,128)}, u32[]{:S(2)}) copy-start(f32[1,4096]{1,0:T(1,128)} %param.12) | copy-start | bytes 49156
  8.2 25.5 %all-to-all-start = ((bf16[8,48,512]{2,1,0:T(8,128)(2,1)}), bf16[8,48,512]{2,1,0:T(8,128)(2,1)S(1)}, u32[]{:S(2)}, u32[]{:S(2)}) async-start(bf16[8,48,512]{2,1,0:T(8,128)(2,1)} %broadcast_in_dim.80), calls=%async_computation | async-start | bytes 786432 | tf_op jit(solution)/shard_map/all_to_all | solution.py:28
  16.9 180.0 %all-gather.2.cloned.1.call-start = ((), (), s32[]{:S(2)}) async-start(), calls=%async_computation.16 | async-start | bytes 3244032 | tf_op jit(solution)/shard_map/all_gather | solution.py:12
  21.6 12.4 %copy-start.11 = (s32[48,8]{1,0:T(8,128)}, s32[48,8]{1,0:T(8,128)S(1)}, u32[]{:S(2)}) copy-start(s32[48,8]{1,0:T(8,128)S(1)} %copy.49) | copy-start | bytes 4612
  34.6 43.1 %copy-start.2 = (bf16[1,1,4096,128]{3,2,1,0:T(8,128)(2,1)S(1)}, bf16[1,1,4096,128]{3,2,1,0:T(8,128)(2,1)}, u32[]{:S(2)}) copy-start(bf16[1,1,4096,128]{3,2,1,0:T(8,128)(2,1)} %param.16) | copy-start | bytes 3145732
  35.9 43.9 %copy-start.1 = (bf16[1,1,4096,128]{3,2,1,0:T(8,128)(2,1)S(1)}, bf16[1,1,4096,128]{3,2,1,0:T(8,128)(2,1)}, u32[]{:S(2)}) copy-start(bf16[1,1,4096,128]{3,2,1,0:T(8,128)(2,1)} %param.17) | copy-start | bytes 3145732
  84.8 35.1 %all-to-all-start.2 = ((bf16[32,3,4096]{2,1,0:T(4,128)(2,1)}), bf16[32,3,4096]{2,1,0:T(4,128)(2,1)}, u32[]{:S(2)}, u32[]{:S(2)}) async-start(bf16[32,3,4096]{2,1,0:T(4,128)(2,1)} %reshape.261), calls=%async_computation.2 | async-start | bytes 2097152 | tf_op jit(solution)/shard_map/all_to_all | solution.py:123
  202.5 19.4 %copy-start.9 = (bf16[3,48,512]{2,1,0:T(8,128)(2,1)S(1)}, bf16[3,48,512]{2,1,0:T(8,128)(2,1)}, u32[]{:S(2)}) copy-start(bf16[3,48,512]{2,1,0:T(8,128)(2,1)} %param.11) | copy-start | bytes 442372
  222.0 2.2 copy-start.17
  222.0 2.2 collective-permute-start
  224.2 0.6 copy-start.3
  225.6 19.1 %all-to-all-start.4 = ((bf16[8,48,512]{2,1,0:T(8,128)(2,1)}), bf16[8,48,512]{2,1,0:T(8,128)(2,1)S(1)}, u32[]{:S(2)}, u32[]{:S(2)}) async-start(bf16[8,48,512]{2,1,0:T(8,128)(2,1)} %broadcast_in_dim.85), calls=%async_computation.4 | async-start | bytes 786432 | tf_op jit(solution)/shard_map/all_to_all | solution.py:28
  244.7 0.7 copy-start.21
  297.6 33.6 %all-to-all-start.6 = ((bf16[32,3,4096]{2,1,0:T(4,128)(2,1)}), bf16[32,3,4096]{2,1,0:T(4,128)(2,1)}, u32[]{:S(2)}, u32[]{:S(2)}) async-start(bf16[32,3,4096]{2,1,0:T(4,128)(2,1)} %reshape.266), calls=%async_computation.6 | async-start | bytes 2097152 | tf_op jit(solution)/shard_map/all_to_all | solution.py:123
  311.7 44.4 %copy-start.4 = (bf16[48,512]{1,0:T(8,128)(2,1)S(1)}, bf16[48,512]{1,0:T(8,128)(2,1)}, u32[]{:S(2)}) copy-start(bf16[48,512]{1,0:T(8,128)(2,1)} %copy-done.3) | copy-start | bytes 147460
  311.7 44.4 %copy-start.18 = (bf16[48,512]{1,0:T(8,128)(2,1)S(1)}, bf16[48,512]{1,0:T(8,128)(2,1)}, u32[]{:S(2)}) copy-start(bf16[48,512]{1,0:T(8,128)(2,1)} %copy-done.17) | copy-start | bytes 147460
  356.7 4.4 copy-start.15
  356.7 2.1 collective-permute-start.1
  359.7 0.6 copy-start.5
  361.1 19.3 %all-to-all-start.8 = ((bf16[8,48,512]{2,1,0:T(8,128)(2,1)}), bf16[8,48,512]{2,1,0:T(8,128)(2,1)S(1)}, u32[]{:S(2)}, u32[]{:S(2)}) async-start(bf16[8,48,512]{2,1,0:T(8,128)(2,1)} %broadcast_in_dim.88), calls=%async_computation.8 | async-start | bytes 786432 | tf_op jit(solution)/shard_map/all_to_all | solution.py:28
  380.3 0.7 copy-start.22
  427.8 33.4 %all-to-all-start.10 = ((bf16[32,3,4096]{2,1,0:T(4,128)(2,1)}), bf16[32,3,4096]{2,1,0:T(4,128)(2,1)}, u32[]{:S(2)}, u32[]{:S(2)}) async-start(bf16[32,3,4096]{2,1,0:T(4,128)(2,1)} %reshape.271), calls=%async_computation.10 | async-start | bytes 2097152 | tf_op jit(solution)/shard_map/all_to_all | solution.py:123
  441.8 41.6 %copy-start.6 = (bf16[48,512]{1,0:T(8,128)(2,1)S(1)}, bf16[48,512]{1,0:T(8,128)(2,1)}, u32[]{:S(2)}) copy-start(bf16[48,512]{1,0:T(8,128)(2,1)} %copy-done.5) | copy-start | bytes 147460
  441.8 41.6 %copy-start.16 = (bf16[48,512]{1,0:T(8,128)(2,1)S(1)}, bf16[48,512]{1,0:T(8,128)(2,1)}, u32[]{:S(2)}) copy-start(bf16[48,512]{1,0:T(8,128)(2,1)} %copy-done.15) | copy-start | bytes 147460
  484.0 4.4 copy-start.19
  484.0 2.1 collective-permute-start.2
  487.0 0.6 copy-start.7
  488.4 19.2 %all-to-all-start.12 = ((bf16[8,48,512]{2,1,0:T(8,128)(2,1)}), bf16[8,48,512]{2,1,0:T(8,128)(2,1)S(1)}, u32[]{:S(2)}, u32[]{:S(2)}) async-start(bf16[8,48,512]{2,1,0:T(8,128)(2,1)} %broadcast_in_dim.91), calls=%async_computation.12 | async-start | bytes 786432 | tf_op jit(solution)/shard_map/all_to_all | solution.py:28
  507.6 0.7 copy-start.23
  551.4 8.6 %copy-start.24 = (f32[48,8]{0,1:T(8,128)S(1)}, f32[48,8]{0,1:T(8,128)}, u32[]{:S(2)}) copy-start(f32[48,8]{0,1:T(8,128)} %get-tuple-element.13) | copy-start | bytes 4612
  551.4 8.6 %copy-start.12 = (s32[48,8]{1,0:T(8,128)S(1)}, s32[48,8]{1,0:T(8,128)}, u32[]{:S(2)}) copy-start(s32[48,8]{1,0:T(8,128)} %copy.61) | copy-start | bytes 4612
  554.5 33.5 %all-to-all-start.14 = ((bf16[32,3,4096]{2,1,0:T(4,128)(2,1)}), bf16[32,3,4096]{2,1,0:T(4,128)(2,1)S(1)}, u32[]{:S(2)}, u32[]{:S(2)}) async-start(bf16[32,3,4096]{2,1,0:T(4,128)(2,1)} %reshape.276), calls=%async_computation.14 | async-start | bytes 2097152 | tf_op jit(solution)/shard_map/all_to_all | solution.py:123
  565.3 42.8 %copy-start.8 = (bf16[48,512]{1,0:T(8,128)(2,1)S(1)}, bf16[48,512]{1,0:T(8,128)(2,1)}, u32[]{:S(2)}) copy-start(bf16[48,512]{1,0:T(8,128)(2,1)} %copy-done.7) | copy-start | bytes 147460
  565.3 42.8 %copy-start.20 = (bf16[48,512]{1,0:T(8,128)(2,1)S(1)}, bf16[48,512]{1,0:T(8,128)(2,1)}, u32[]{:S(2)}) copy-start(bf16[48,512]{1,0:T(8,128)(2,1)} %copy-done.19) | copy-start | bytes 147460
  565.3 42.9 %copy-start.13 = (bf16[1,48,512]{2,1,0:T(8,128)(2,1)S(1)}, bf16[1,48,512]{2,1,0:T(8,128)(2,1)}, u32[]{:S(2)}) copy-start(bf16[1,48,512]{2,1,0:T(8,128)(2,1)} %get-tuple-element.5) | copy-start | bytes 147460
  565.3 42.9 %copy-start.14 = (bf16[1,48,512]{2,1,0:T(8,128)(2,1)S(1)}, bf16[1,48,512]{2,1,0:T(8,128)(2,1)}, u32[]{:S(2)}) copy-start(bf16[1,48,512]{2,1,0:T(8,128)(2,1)} %get-tuple-element.7) | copy-start | bytes 147460
Sparse Core Ops, SparseCore 0:
  20.2 176.5 all-gather.1
where the time goes:
time: 619 us; the launch traced here: 616 us
  blocking collectives  221 us (36%)
  waiting for transfers between devices  212 us (34%)
  local copies, waits for them, and re-layouts  51.6 us (8%)
  matrix products  51.2 us (8%)
  starting transfers between devices  47.8 us (8%)
  other arithmetic  18.6 us (3%)
  between operations  13.9 us (2%)
    all_to_all x4, blocking collectives, per_device(): lax.all_to_all(outgoing, 'expert', split_axis=0, concat_axis=0, tiled=True)  147 us
    all_to_all x4, waiting for transfers between devices, per_device(): lax.all_to_all(outcome, 'expert', split_axis=0, concat_axis=0, tiled=True)  84.1 us
    all_gather x1, waiting for transfers between devices, turned_gather(): filled, at, outs = (lax.all_gather(both, axis, axis=0, tiled=True), 0, [])  74.5 us
    all_to_all x4, blocking collectives, sent_and_summed(): lax.all_to_all(blocks, axis, split_axis=0, concat_axis=0, tiled=True)  74.1 us
    all_to_all x4, waiting for transfers between devices, from_everyone(): return lax.all_to_all(copies, axis, split_axis=0, concat_axis=0, tiled=True)  50.4 us
    dot_general x20, matrix products, product(): return jnp.dot(left, right, preferred_element_type=jnp.float32)  44.9 us
    all_to_all x4, starting transfers between devices, per_device(): lax.all_to_all(outcome, 'expert', split_axis=0, concat_axis=0, tiled=True)  24.7 us
    all_to_all x4, starting transfers between devices, from_everyone(): return lax.all_to_all(copies, axis, split_axis=0, concat_axis=0, tiled=True)  19.2 us
  transfers between devices with their start and end apart: 12, of which 12 were waited for; matrix products, arithmetic and copies ran while one was open for 9% of the time, Pallas kernels for 0%

commit v1 on v0

--- a/solution.py
+++ b/solution.py
@@ -6,10 +6,23 @@
 CAP = 3
 
 
+def report_the_slots(peer_axis, z_in):
+    now = jnp.concatenate(
+        lax.all_to_all(
+            jnp.stack([z_in for _ in range(lax.axis_size(peer_axis))], 0),
+            peer_axis,
+            split_axis=0,
+            concat_axis=0,
+        ),
+        0,
+    )
+    return now
+
+
 def turned_gather(arrays, axis, dims):
     turned = [jnp.moveaxis(a, dim, 0) for a, dim in zip(arrays, dims)]
     both = jnp.concatenate([t.reshape(len(t), -1) for t in turned], axis=1)
-    filled, at, outs = (lax.all_gather(both, axis, axis=0, tiled=True), 0, [])
+    filled, at, outs = (report_the_slots(axis, both), 0, [])
     for t, dim in zip(turned, dims):
         share = filled[:, at : at + t[0].size].reshape(-1, *t.shape[1:])
         outs.append(jnp.moveaxis(share, 0, dim))

time: 619 us -> 646 us (1.044)
  blocking collectives: 221 us -> 253 us
  between operations: 13.9 us -> 0.48 us
    all_to_all x0 -> x1, waiting for transfers between devices: none -> 75.6 us  [report_the_slots(): lax.all_to_all(jnp.stack([z_in for _ in range(lax.axis_size(peer_axis))],...]
    all_gather x1 -> x0, waiting for transfers between devices: 74.5 us -> none  [turned_gather(): filled, at, outs = (lax.all_gather(both, axis, axis=0, tiled=True), 0, [])]
    all_to_all x4, blocking collectives: 74.1 us -> 105 us  [sent_and_summed(): lax.all_to_all(blocks, axis, split_axis=0, concat_axis=0, tiled=True)]
  transfers between devices with their start and end apart: 12 -> 12, of which waited for: 12 -> 12; matrix products, arithmetic and copies ran while one was open for 9% -> 7% of each run, Pallas kernels for 0% -> 0%
where the time goes in v1:
time: 646 us; the launch traced here: 643 us
  blocking collectives  253 us (39%)
  waiting for transfers between devices  214 us (33%)
  local copies, waits for them, and re-layouts  57.5 us (9%)
  matrix products  49.7 us (8%)
  starting transfers between devices  49.2 us (8%)
  other arithmetic  18.7 us (3%)
    all_to_all x4, blocking collectives, per_device(): lax.all_to_all(outgoing, 'expert', split_axis=0, concat_axis=0, tiled=True)  148 us
    all_to_all x4, blocking collectives, sent_and_summed(): lax.all_to_all(blocks, axis, split_axis=0, concat_axis=0, tiled=True)  105 us
    all_to_all x4, waiting for transfers between devices, per_device(): lax.all_to_all(outcome, 'expert', split_axis=0, concat_axis=0, tiled=True)  84.8 us
    all_to_all x1, waiting for transfers between devices, report_the_slots(): lax.all_to_all(jnp.stack([z_in for _ in range(lax.axis_size(peer_axis))],...  75.6 us
    all_to_all x4, waiting for transfers between devices, from_everyone(): return lax.all_to_all(copies, axis, split_axis=0, concat_axis=0, tiled=True)  51.1 us
    dot_general x20, matrix products, product(): return jnp.dot(left, right, preferred_element_type=jnp.float32)  43.4 us
    all_to_all x4, starting transfers between devices, per_device(): lax.all_to_all(outcome, 'expert', split_axis=0, concat_axis=0, tiled=True)  21 us
    all_to_all x4, starting transfers between devices, from_everyone(): return lax.all_to_all(copies, axis, split_axis=0, concat_axis=0, tiled=True)  19 us
  transfers between devices with their start and end apart: 12, of which 12 were waited for; matrix products, arithmetic and copies ran while one was open for 7% of the time, Pallas kernels for 0%

profile of v1, /device:TPU:72, one launch (start us, length us, event | category | flops | bytes accessed | tf_op | source)
XLA Modules:
  0.0 642.5 jit_solution(14029251951786205473)
XLA Ops:
  1.7 8.7 %all-to-all-start = ((bf16[8,48,512]{2,1,0:T(8,128)(2,1)}), bf16[8,48,512]{2,1,0:T(8,128)(2,1)S(1)}, u32[]{:S(2)}, u32[]{:S(2)}) async-start(bf16[8,48,512]{2,1,0:T(8,128)(2,1)} %broadcast_in_dim.80), calls=%async_computation | async-start | bytes 786432 | tf_op jit(solution)/shard_map/all_to_all | solution.py:41
  12.0 15.2 %all-to-all-done = bf16[8,48,512]{2,1,0:T(8,128)(2,1)S(1)} async-done(((bf16[8,48,512]{2,1,0:T(8,128)(2,1)}), bf16[8,48,512]{2,1,0:T(8,128)(2,1)S(1)}, u32[]{:S(2)}, u32[]{:S(2)}) %all-to-all-start) | async-done | bytes 393248 | tf_op jit(solution)/shard_map/all_to_all | solution.py:41
  29.4 39.2 %all_to_all.85 = bf16[32,3,4096]{2,1,0:T(4,128)(2,1)} all-to-all(bf16[32,3,4096]{2,1,0:T(4,128)(2,1)} %reshape.265), channel_id=1, replica_groups=mesh['pipe'=2,'tensor'=8,'expert'=32] {'expert'}, dimensions={0} | all-to-all | bytes 1572864 | tf_op jit(solution)/shard_map/all_to_all | solution.py:125
  68.6 2.5 reshape.266
  71.1 2.1 fusion.34
  73.2 2.7 convolution_convert_fusion.3
  75.9 2.3 reshape.267
  78.2 5.4 all-to-all-start.3
  83.6 1.5 copy.51
  88.0 1.6 copy.52
  89.6 22.2 %all-to-all-done.3 = bf16[32,3,4096]{2,1,0:T(4,128)(2,1)} async-done(((bf16[32,3,4096]{2,1,0:T(4,128)(2,1)}), bf16[32,3,4096]{2,1,0:T(4,128)(2,1)}, u32[]{:S(2)}, u32[]{:S(2)}) %all-to-all-start.3) | async-done | bytes 786464 | tf_op jit(solution)/shard_map/all_to_all | solution.py:136
  111.8 3.0 stack.10
  114.8 5.3 all-to-all-start.1
  122.9 1.5 select_reduce_fusion.3
  124.4 2.5 reshape.268
  126.9 75.6 %all-to-all-done.1 = bf16[32,128,384]{2,1,0:T(8,128)(2,1)} async-done(((bf16[32,128,384]{2,1,0:T(8,128)(2,1)}), bf16[32,128,384]{2,1,0:T(8,128)(2,1)}, u32[]{:S(2)}, u32[]{:S(2)}) %all-to-all-start.1) | async-done | bytes 3145760 | tf_op jit(solution)/shard_map/all_to_all | solution.py:11
  202.5 2.1 fusion.58
  204.7 3.1 fusion.15
  207.8 1.7 fusion
  209.5 51.1 %all_to_all.86 = bf16[8,48,512]{2,1,0:T(8,128)(2,1)S(1)} all-to-all(bf16[8,48,512]{2,1,0:T(8,128)(2,1)S(1)} %bitcast.151), channel_id=1, replica_groups=mesh['pipe'=2,'tensor'=8,'expert'=32] {'tensor'}, dimensions={0} | all-to-all | bytes 786432 | tf_op jit(solution)/shard_map/all_to_all | solution.py:56
  264.3 3.5 all-to-all-start.5
  270.6 10.5 %all-to-all-done.5 = bf16[8,48,512]{2,1,0:T(8,128)(2,1)S(1)} async-done(((bf16[8,48,512]{2,1,0:T(8,128)(2,1)}), bf16[8,48,512]{2,1,0:T(8,128)(2,1)S(1)}, u32[]{:S(2)}, u32[]{:S(2)}) %all-to-all-start.5) | async-done | bytes 393248 | tf_op jit(solution)/shard_map/all_to_all | solution.py:41
  283.1 2.3 reshape.270
  285.3 38.2 %all_to_all.87 = bf16[32,3,4096]{2,1,0:T(4,128)(2,1)} all-to-all(bf16[32,3,4096]{2,1,0:T(4,128)(2,1)} %reshape.270), channel_id=1, replica_groups=mesh['pipe'=2,'tensor'=8,'expert'=32] {'expert'}, dimensions={0} | all-to-all | bytes 1572864 | tf_op jit(solution)/shard_map/all_to_all | solution.py:125
  323.5 2.5 reshape.271
  326.0 2.1 fusion.32
  328.1 2.7 convolution_convert_fusion.2
  330.8 2.3 reshape.272
  333.1 4.6 all-to-all-start.7
  339.1 1.5 select_reduce_fusion.2
  340.6 2.1 fusion.56
  342.7 3.2 fusion.14
  345.9 19.7 %all-to-all-done.7 = bf16[32,3,4096]{2,1,0:T(4,128)(2,1)} async-done(((bf16[32,3,4096]{2,1,0:T(4,128)(2,1)}), bf16[32,3,4096]{2,1,0:T(4,128)(2,1)}, u32[]{:S(2)}, u32[]{:S(2)}) %all-to-all-start.7) | async-done | bytes 786464 | tf_op jit(solution)/shard_map/all_to_all | solution.py:136
  365.6 2.5 reshape.273
  368.0 1.6 fusion.1
  369.7 18.5 %all_to_all.88 = bf16[8,48,512]{2,1,0:T(8,128)(2,1)S(1)} all-to-all(bf16[8,48,512]{2,1,0:T(8,128)(2,1)S(1)} %bitcast.152), channel_id=1, replica_groups=mesh['pipe'=2,'tensor'=8,'expert'=32] {'tensor'}, dimensions={0} | all-to-all | bytes 786432 | tf_op jit(solution)/shard_map/all_to_all | solution.py:56
  393.3 3.5 all-to-all-start.9
  399.6 12.6 %all-to-all-done.9 = bf16[8,48,512]{2,1,0:T(8,128)(2,1)S(1)} async-done(((bf16[8,48,512]{2,1,0:T(8,128)(2,1)}), bf16[8,48,512]{2,1,0:T(8,128)(2,1)S(1)}, u32[]{:S(2)}, u32[]{:S(2)}) %all-to-all-start.9) | async-done | bytes 393248 | tf_op jit(solution)/shard_map/all_to_all | solution.py:41
  414.2 2.3 reshape.275
  416.5 35.1 %all_to_all.89 = bf16[32,3,4096]{2,1,0:T(4,128)(2,1)} all-to-all(bf16[32,3,4096]{2,1,0:T(4,128)(2,1)} %reshape.275), channel_id=1, replica_groups=mesh['pipe'=2,'tensor'=8,'expert'=32] {'expert'}, dimensions={0} | all-to-all | bytes 1572864 | tf_op jit(solution)/shard_map/all_to_all | solution.py:125
  451.5 2.5 reshape.276
  454.0 2.1 fusion.30
  456.1 2.7 convolution_convert_fusion.1
  458.8 2.3 reshape.277
  461.1 5.6 all-to-all-start.11
  468.1 1.5 select_reduce_fusion.1
  469.6 2.1 fusion.54
  471.8 3.2 fusion.13
  475.0 19.9 %all-to-all-done.11 = bf16[32,3,4096]{2,1,0:T(4,128)(2,1)} async-done(((bf16[32,3,4096]{2,1,0:T(4,128)(2,1)}), bf16[32,3,4096]{2,1,0:T(4,128)(2,1)}, u32[]{:S(2)}, u32[]{:S(2)}) %all-to-all-start.11) | async-done | bytes 786464 | tf_op jit(solution)/shard_map/all_to_all | solution.py:136
  494.8 2.5 reshape.278
  497.3 1.6 fusion.2
  499.0 17.9 %all_to_all.90 = bf16[8,48,512]{2,1,0:T(8,128)(2,1)S(1)} all-to-all(bf16[8,48,512]{2,1,0:T(8,128)(2,1)S(1)} %bitcast.153), channel_id=1, replica_groups=mesh['pipe'=2,'tensor'=8,'expert'=32] {'tensor'}, dimensions={0} | all-to-all | bytes 786432 | tf_op jit(solution)/shard_map/all_to_all | solution.py:56
  521.9 3.5 all-to-all-start.13
  528.2 12.9 %all-to-all-done.13 = bf16[8,48,512]{2,1,0:T(8,128)(2,1)S(1)} async-done(((bf16[8,48,512]{2,1,0:T(8,128)(2,1)}), bf16[8,48,512]{2,1,0:T(8,128)(2,1)S(1)}, u32[]{:S(2)}, u32[]{:S(2)}) %all-to-all-start.13) | async-done | bytes 393248 | tf_op jit(solution)/shard_map/all_to_all | solution.py:41
  543.1 2.3 reshape.280
  545.4 35.1 %all_to_all.91 = bf16[32,3,4096]{2,1,0:T(4,128)(2,1)} all-to-all(bf16[32,3,4096]{2,1,0:T(4,128)(2,1)} %reshape.280), channel_id=1, replica_groups=mesh['pipe'=2,'tensor'=8,'expert'=32] {'expert'}, dimensions={0} | all-to-all | bytes 1572864 | tf_op jit(solution)/shard_map/all_to_all | solution.py:125
  580.5 2.5 reshape.281
  582.9 2.1 fusion.28
  585.1 1.8 convolution_convert_fusion
  588.2 5.4 all-to-all-start.15
  593.9 1.5 fusion.52
  595.4 3.2 fusion.12
  598.6 23.1 %all-to-all-done.15 = bf16[32,3,4096]{2,1,0:T(4,128)(2,1)S(1)} async-done(((bf16[32,3,4096]{2,1,0:T(4,128)(2,1)}), bf16[32,3,4096]{2,1,0:T(4,128)(2,1)S(1)}, u32[]{:S(2)}, u32[]{:S(2)}) %all-to-all-start.15) | async-done | bytes 786464 | tf_op jit(solution)/shard_map/all_to_all | solution.py:136
  623.9 17.9 %all_to_all.92 = bf16[8,48,512]{2,1,0:T(8,128)(2,1)S(1)} all-to-all(bf16[8,48,512]{2,1,0:T(8,128)(2,1)S(1)} %bitcast.154), channel_id=1, replica_groups=mesh['pipe'=2,'tensor'=8,'expert'=32] {'tensor'}, dimensions={0} | all-to-all | bytes 786432 | tf_op jit(solution)/shard_map/all_to_all | solution.py:56
  (122 shorter events, 46.5 us)
Async XLA Ops:
  0.0 73.2 %copy-start = (bf16[1,1,128,4096]{3,2,1,0:T(8,128)(2,1)S(1)}, bf16[1,1,128,4096]{3,2,1,0:T(8,128)(2,1)}, u32[]{:S(2)}) copy-start(bf16[1,1,128,4096]{3,2,1,0:T(8,128)(2,1)} %param.18) | copy-start | bytes 3145732
  0.0 27.5 %copy-start.10 = (f32[1,4096]{1,0:T(1,128)S(1)}, f32[1,4096]{1,0:T(1,128)}, u32[]{:S(2)}) copy-start(f32[1,4096]{1,0:T(1,128)} %param.12) | copy-start | bytes 49156
  1.7 25.5 %all-to-all-start = ((bf16[8,48,512]{2,1,0:T(8,128)(2,1)}), bf16[8,48,512]{2,1,0:T(8,128)(2,1)S(1)}, u32[]{:S(2)}, u32[]{:S(2)}) async-start(bf16[8,48,512]{2,1,0:T(8,128)(2,1)} %broadcast_in_dim.80), calls=%async_computation | async-start | bytes 786432 | tf_op jit(solution)/shard_map/all_to_all | solution.py:41
  11.9 15.7 %copy-start.11 = (s32[48,8]{1,0:T(8,128)}, s32[48,8]{1,0:T(8,128)S(1)}, u32[]{:S(2)}) copy-start(s32[48,8]{1,0:T(8,128)S(1)} %copy.53) | copy-start | bytes 4612
  28.1 43.0 %copy-start.2 = (bf16[1,1,4096,128]{3,2,1,0:T(8,128)(2,1)S(1)}, bf16[1,1,4096,128]{3,2,1,0:T(8,128)(2,1)}, u32[]{:S(2)}) copy-start(bf16[1,1,4096,128]{3,2,1,0:T(8,128)(2,1)} %param.16) | copy-start | bytes 3145732
  29.4 43.8 %copy-start.1 = (bf16[1,1,4096,128]{3,2,1,0:T(8,128)(2,1)S(1)}, bf16[1,1,4096,128]{3,2,1,0:T(8,128)(2,1)}, u32[]{:S(2)}) copy-start(bf16[1,1,4096,128]{3,2,1,0:T(8,128)(2,1)} %param.17) | copy-start | bytes 3145732
  78.2 33.6 %all-to-all-start.3 = ((bf16[32,3,4096]{2,1,0:T(4,128)(2,1)}), bf16[32,3,4096]{2,1,0:T(4,128)(2,1)}, u32[]{:S(2)}, u32[]{:S(2)}) async-start(bf16[32,3,4096]{2,1,0:T(4,128)(2,1)} %reshape.267), calls=%async_computation.3 | async-start | bytes 2097152 | tf_op jit(solution)/shard_map/all_to_all | solution.py:136
  114.8 87.7 %all-to-all-start.1 = ((bf16[32,128,384]{2,1,0:T(8,128)(2,1)}), bf16[32,128,384]{2,1,0:T(8,128)(2,1)}, u32[]{:S(2)}, u32[]{:S(2)}) async-start(bf16[32,128,384]{2,1,0:T(8,128)(2,1)} %stack.10), calls=%async_computation.1 | async-start | bytes 6291456 | tf_op jit(solution)/shard_map/all_to_all | solution.py:11
  207.8 52.9 %copy-start.9 = (bf16[3,48,512]{2,1,0:T(8,128)(2,1)S(1)}, bf16[3,48,512]{2,1,0:T(8,128)(2,1)}, u32[]{:S(2)}) copy-start(bf16[3,48,512]{2,1,0:T(8,128)(2,1)} %param.11) | copy-start | bytes 442372
  260.7 2.2 copy-start.17
  260.7 2.2 collective-permute-start
  262.9 0.6 copy-start.3
  264.3 16.8 %all-to-all-start.5 = ((bf16[8,48,512]{2,1,0:T(8,128)(2,1)}), bf16[8,48,512]{2,1,0:T(8,128)(2,1)S(1)}, u32[]{:S(2)}, u32[]{:S(2)}) async-start(bf16[8,48,512]{2,1,0:T(8,128)(2,1)} %broadcast_in_dim.85), calls=%async_computation.5 | async-start | bytes 786432 | tf_op jit(solution)/shard_map/all_to_all | solution.py:41
  281.1 0.7 copy-start.21
  333.1 32.5 %all-to-all-start.7 = ((bf16[32,3,4096]{2,1,0:T(4,128)(2,1)}), bf16[32,3,4096]{2,1,0:T(4,128)(2,1)}, u32[]{:S(2)}, u32[]{:S(2)}) async-start(bf16[32,3,4096]{2,1,0:T(4,128)(2,1)} %reshape.272), calls=%async_computation.7 | async-start | bytes 2097152 | tf_op jit(solution)/shard_map/all_to_all | solution.py:136
  345.9 42.4 %copy-start.4 = (bf16[48,512]{1,0:T(8,128)(2,1)S(1)}, bf16[48,512]{1,0:T(8,128)(2,1)}, u32[]{:S(2)}) copy-start(bf16[48,512]{1,0:T(8,128)(2,1)} %copy-done.3) | copy-start | bytes 147460
  345.9 42.4 %copy-start.18 = (bf16[48,512]{1,0:T(8,128)(2,1)S(1)}, bf16[48,512]{1,0:T(8,128)(2,1)}, u32[]{:S(2)}) copy-start(bf16[48,512]{1,0:T(8,128)(2,1)} %copy-done.17) | copy-start | bytes 147460
  389.0 4.3 copy-start.15
  389.0 2.1 collective-permute-start.1
  391.9 0.6 copy-start.5
  393.3 18.9 %all-to-all-start.9 = ((bf16[8,48,512]{2,1,0:T(8,128)(2,1)}), bf16[8,48,512]{2,1,0:T(8,128)(2,1)S(1)}, u32[]{:S(2)}, u32[]{:S(2)}) async-start(bf16[8,48,512]{2,1,0:T(8,128)(2,1)} %broadcast_in_dim.88), calls=%async_computation.9 | async-start | bytes 786432 | tf_op jit(solution)/shard_map/all_to_all | solution.py:41
  412.2 0.7 copy-start.22
  461.1 33.7 %all-to-all-start.11 = ((bf16[32,3,4096]{2,1,0:T(4,128)(2,1)}), bf16[32,3,4096]{2,1,0:T(4,128)(2,1)}, u32[]{:S(2)}, u32[]{:S(2)}) async-start(bf16[32,3,4096]{2,1,0:T(4,128)(2,1)} %reshape.277), calls=%async_computation.11 | async-start | bytes 2097152 | tf_op jit(solution)/shard_map/all_to_all | solution.py:136
  475.0 42.0 %copy-start.6 = (bf16[48,512]{1,0:T(8,128)(2,1)S(1)}, bf16[48,512]{1,0:T(8,128)(2,1)}, u32[]{:S(2)}) copy-start(bf16[48,512]{1,0:T(8,128)(2,1)} %copy-done.5) | copy-start | bytes 147460
  475.0 42.0 %copy-start.16 = (bf16[48,512]{1,0:T(8,128)(2,1)S(1)}, bf16[48,512]{1,0:T(8,128)(2,1)}, u32[]{:S(2)}) copy-start(bf16[48,512]{1,0:T(8,128)(2,1)} %copy-done.15) | copy-start | bytes 147460
  517.6 4.3 copy-start.19
  517.6 2.1 collective-permute-start.2
  520.5 0.6 copy-start.7
  521.9 19.2 %all-to-all-start.13 = ((bf16[8,48,512]{2,1,0:T(8,128)(2,1)}), bf16[8,48,512]{2,1,0:T(8,128)(2,1)S(1)}, u32[]{:S(2)}, u32[]{:S(2)}) async-start(bf16[8,48,512]{2,1,0:T(8,128)(2,1)} %broadcast_in_dim.91), calls=%async_computation.13 | async-start | bytes 786432 | tf_op jit(solution)/shard_map/all_to_all | solution.py:41
  541.1 0.7 copy-start.23
  585.1 8.6 %copy-start.24 = (f32[48,8]{0,1:T(8,128)S(1)}, f32[48,8]{0,1:T(8,128)}, u32[]{:S(2)}) copy-start(f32[48,8]{0,1:T(8,128)} %get-tuple-element.13) | copy-start | bytes 4612
  585.1 8.7 %copy-start.12 = (s32[48,8]{1,0:T(8,128)S(1)}, s32[48,8]{1,0:T(8,128)}, u32[]{:S(2)}) copy-start(s32[48,8]{1,0:T(8,128)} %copy.65) | copy-start | bytes 4612
  588.2 33.5 %all-to-all-start.15 = ((bf16[32,3,4096]{2,1,0:T(4,128)(2,1)}), bf16[32,3,4096]{2,1,0:T(4,128)(2,1)S(1)}, u32[]{:S(2)}, u32[]{:S(2)}) async-start(bf16[32,3,4096]{2,1,0:T(4,128)(2,1)} %reshape.282), calls=%async_computation.15 | async-start | bytes 2097152 | tf_op jit(solution)/shard_map/all_to_all | solution.py:136
  598.6 43.2 %copy-start.8 = (bf16[48,512]{1,0:T(8,128)(2,1)S(1)}, bf16[48,512]{1,0:T(8,128)(2,1)}, u32[]{:S(2)}) copy-start(bf16[48,512]{1,0:T(8,128)(2,1)} %copy-done.7) | copy-start | bytes 147460
  598.6 43.2 %copy-start.20 = (bf16[48,512]{1,0:T(8,128)(2,1)S(1)}, bf16[48,512]{1,0:T(8,128)(2,1)}, u32[]{:S(2)}) copy-start(bf16[48,512]{1,0:T(8,128)(2,1)} %copy-done.19) | copy-start | bytes 147460
  598.6 43.3 %copy-start.13 = (bf16[1,48,512]{2,1,0:T(8,128)(2,1)S(1)}, bf16[1,48,512]{2,1,0:T(8,128)(2,1)}, u32[]{:S(2)}) copy-start(bf16[1,48,512]{2,1,0:T(8,128)(2,1)} %get-tuple-element.5) | copy-start | bytes 147460
  598.6 43.3 %copy-start.14 = (bf16[1,48,512]{2,1,0:T(8,128)(2,1)S(1)}, bf16[1,48,512]{2,1,0:T(8,128)(2,1)}, u32[]{:S(2)}) copy-start(bf16[1,48,512]{2,1,0:T(8,128)(2,1)} %get-tuple-element.7) | copy-start | bytes 147460
